TPU v7x, 32 devices: a whole 2x2x4 slice. The times are simulated.
32 devices in a mesh: shard: 8 (over z, y), model: 4 (over x, core).
Axes of the slice: x: 2, y: 2, z: 4, core: 2. Of those that a mesh axis runs over, the one named last changes fastest.
Arguments:
- w_query: bfloat16 [12288, 12288], P('shard', 'model'), may hold values from -0.078125 to 0.078125
- low_query: bfloat16 [12288, 16], P('shard'), may hold values from -0.0546875 to 0.0546875
- high_query: bfloat16 [16, 12288], P(None, 'model'), may hold values from -1.5 to 1.5
- w_key: bfloat16 [12288, 12288], P('shard', 'model'), may hold values from -0.078125 to 0.078125
- low_key: bfloat16 [12288, 16], P('shard'), may hold values from -0.0546875 to 0.0546875
- high_key: bfloat16 [16, 12288], P(None, 'model'), may hold values from -1.5 to 1.5
- w_value: bfloat16 [12288, 12288], P('shard', 'model'), may hold values from -0.078125 to 0.078125
- low_value: bfloat16 [12288, 16], P('shard'), may hold values from -0.0546875 to 0.0546875
- high_value: bfloat16 [16, 12288], P(None, 'model'), may hold values from -1.5 to 1.5
- norm_gain: float32 [12288], P('shard'), may hold values from 0.25 to 1.75
Outputs:
- final_query: bfloat16 [12288, 12288], P(None, ('model', 'shard'))
- final_key: bfloat16 [12288, 12288], P(None, ('model', 'shard'))
- final_value: bfloat16 [12288, 12288], P(None, ('model', 'shard'))
- scale_query: float32 [12288], P(('model', 'shard'))
- scale_key: float32 [12288], P(('model', 'shard'))
- scale_value: float32 [12288], P(('model', 'shard'))
All inputs are finite; a program needn't handle non-finite values. Where the computation divides by a largest or mean magnitude, that divisor is 1e-20 or more.
Results may differ from a plain program's by a relative error of at most 0.001.
Values may be sent and summed in bfloat16 or wider, within the bound.
A program may use at most 192 MiB of HBM per device.

v0:
```python
import jax
import jax.numpy as jnp
from jax import lax
from jax.sharding import PartitionSpec as P

mix_rate = 1.0


def on_device(
    w_query,
    low_query,
    high_query,
    w_key,
    low_key,
    high_key,
    w_value,
    low_value,
    high_value,
    norm_gain,
):
    result_query = w_query.astype(jnp.float32) + mix_rate * jnp.dot(
        low_query, high_query, preferred_element_type=jnp.float32
    )
    result_key = w_key.astype(jnp.float32) + mix_rate * jnp.dot(
        low_key, high_key, preferred_element_type=jnp.float32
    )
    result_value = w_value.astype(jnp.float32) + mix_rate * jnp.dot(
        low_value, high_value, preferred_element_type=jnp.float32
    )
    result_gained_query = result_query * norm_gain[:, None]
    result_gained_key = result_key * norm_gain[:, None]
    result_gained_value = result_value * norm_gain[:, None]
    scale_query, scale_key, scale_value = lax.pmax(
        (
            jnp.max(jnp.abs(result_gained_query), axis=0),
            jnp.max(jnp.abs(result_gained_key), axis=0),
            jnp.max(jnp.abs(result_gained_value), axis=0),
        ),
        "shard",
    )
    narrow_query, narrow_key, narrow_value = (
        (result_gained_query / scale_query).astype(jnp.bfloat16),
        (result_gained_key / scale_key).astype(jnp.bfloat16),
        (result_gained_value / scale_value).astype(jnp.bfloat16),
    )
    final_query, final_key, final_value = (
        lax.all_to_all(narrow_query, "shard", split_axis=1, concat_axis=0, tiled=True),
        lax.all_to_all(narrow_key, "shard", split_axis=1, concat_axis=0, tiled=True),
        lax.all_to_all(narrow_value, "shard", split_axis=1, concat_axis=0, tiled=True),
    )
    place = lax.axis_index("shard")
    scale_query = lax.dynamic_slice_in_dim(
        scale_query, place * final_query.shape[1], final_query.shape[1]
    )
    scale_key = lax.dynamic_slice_in_dim(scale_key, place * final_key.shape[1], final_key.shape[1])
    scale_value = lax.dynamic_slice_in_dim(
        scale_value, place * final_value.shape[1], final_value.shape[1]
    )
    return (final_query, final_key, final_value, scale_query, scale_key, scale_value)


def solution(mesh):
    return jax.shard_map(
        on_device,
        mesh=mesh,
        in_specs=(
            P("shard", "model"),
            P("shard", None),
            P(None, "model"),
            P("shard", "model"),
            P("shard", None),
            P(None, "model"),
            P("shard", "model"),
            P("shard", None),
            P(None, "model"),
            P("shard"),
        ),
        out_specs=(
            P(None, ("model", "shard")),
            P(None, ("model", "shard")),
            P(None, ("model", "shard")),
            P(("model", "shard")),
            P(("model", "shard")),
            P(("model", "shard")),
        ),
        check_vma=False,
    )
```

profile of v0, /device:TPU:0, one launch (start us, length us, event | category | flops | bytes accessed | tf_op | source)
XLA Modules:
  0.0 740.9 jit_solution(7890613569217903696)
XLA Ops:
  0.6 0.0 copy-start
  0.7 0.0 copy-start.3
  0.7 0.0 copy-start.4
  0.7 0.0 copy-start.6
  0.7 0.0 copy-start.2
  0.7 0.8 copy-done
  1.5 13.5 %abs_reduce_fusion.2 = (f32[3072]{0:T(1024)S(1)}, f32[1536,3072]{1,0:T(8,128)}) fusion(f32[1536]{0:T(1024)} %param.19, bf16[1536,16]{0,1:T(8,128)(2,1)} %param.11, bf16[16,3072]{1,0:T(8,128)(2,1)S(1)} %copy-done, bf16[1536,3072]{1,0:T(8,128)(2,1)} %param.10), kind=kOutput, calls=%fused_computation.7 | convolution fusion | flops 174584832 | bytes 28477440 | tf_op jit(solution)/shard_map/dot_general | solution.py:21
  15.0 0.0 copy-done.3
  15.0 0.0 copy-done.6
  15.1 0.0 slice-start.2
  15.1 0.0 copy-start.5
  15.1 0.0 copy-start.7
  15.1 8.0 %abs_reduce_fusion.1 = (f32[3072]{0:T(1024)S(1)}, f32[1536,3072]{1,0:T(8,128)}) fusion(f32[1536]{0:T(1024)S(1)} %copy-done.3, bf16[1536,16]{0,1:T(8,128)(2,1)S(1)} %copy-done.4, bf16[16,3072]{1,0:T(8,128)(2,1)S(1)} %copy-done.6, bf16[1536,3072]{1,0:T(8,128)(2,1)S(1)} %copy-done.2), kind=kOutput, calls=%fused_computation.4 | convolution fusion | flops 174584832 | bytes 28477440 | tf_op jit(solution)/shard_map/dot_general | solution.py:24
  23.1 8.0 %abs_reduce_fusion = (f32[3072]{0:T(1024)S(1)}, f32[1536,3072]{1,0:T(8,128)}) fusion(f32[1536]{0:T(1024)S(1)} %copy-done.3, bf16[1536,16]{0,1:T(8,128)(2,1)S(1)} %copy-done.5, bf16[16,3072]{1,0:T(8,128)(2,1)S(1)} %copy-done.7, bf16[1536,3072]{1,0:T(8,128)(2,1)S(1)} %bitcast.34), kind=kOutput, calls=%fused_computation.1 | convolution fusion | flops 174584832 | bytes 28477440 | tf_op jit(solution)/shard_map/dot_general | solution.py:27
  31.1 39.2 %all-reduce = (f32[3072]{0:T(1024)S(1)}, f32[3072]{0:T(1024)S(1)}, f32[3072]{0:T(1024)S(1)}) all-reduce(f32[3072]{0:T(1024)S(1)} %get-tuple-element.9, f32[3072]{0:T(1024)S(1)} %get-tuple-element.11, f32[3072]{0:T(1024)S(1)} %get-tuple-element.13), channel_id=1, replica_groups=mesh['shard'=8,'model'=4] {'shard'}, use_global_device_ids=true, to_apply=%region_1.0 | all-reduce | flops 9216 | bytes 73728 | tf_op jit(solution)/shard_map/pmax | solution.py:33
  70.2 11.5 %divide_convert_fusion.2 = bf16[1536,3072]{1,0:T(8,128)(2,1)} fusion(f32[1536,3072]{1,0:T(8,128)} %get-tuple-element.10, f32[3072]{0:T(1024)S(1)} %get-tuple-element.6), kind=kLoop, calls=%fused_computation.6 | loop fusion | flops 9437184 | bytes 28323840 | tf_op jit(solution)/shard_map/convert_element_type | solution.py:42
  81.8 8.4 %copy.30 = bf16[192,8,8,384]{3,2,0,1:T(8,128)(2,1)} copy(bf16[192,8,8,384]{3,2,1,0:T(8,128)(2,1)} %bitcast.32) | data formatting | bytes 18874368 | tf_op jit(solution)/shard_map/all_to_all | solution.py:47
  90.2 5.1 all-to-all-start
  95.3 20.3 %divide_convert_fusion = (bf16[1536,3072]{1,0:T(8,128)(2,1)}, bf16[1536,3072]{1,0:T(8,128)(2,1)}) fusion(f32[1536,3072]{1,0:T(8,128)} %get-tuple-element.14, f32[3072]{0:T(1024)S(1)} %get-tuple-element.8, f32[1536,3072]{1,0:T(8,128)} %get-tuple-element.12, f32[3072]{0:T(1024)S(1)} %get-tuple-element.7), kind=kLoop, calls=%fused_computation | loop fusion | flops 18874368 | bytes 56647680 | tf_op jit(solution)/shard_map/convert_element_type | solution.py:44
  115.6 8.3 %copy.29 = bf16[192,8,8,384]{3,2,0,1:T(8,128)(2,1)} copy(bf16[192,8,8,384]{3,2,1,0:T(8,128)(2,1)} %bitcast.31) | data formatting | bytes 18874368 | tf_op jit(solution)/shard_map/all_to_all | solution.py:48
  124.0 169.9 %all-to-all-done = bf16[1536,8,384]{2,0,1:T(8,128)(2,1)} async-done(((bf16[1536,8,384]{2,0,1:T(8,128)(2,1)}), bf16[1536,8,384]{2,0,1:T(8,128)(2,1)}, u32[]{:S(2)}, u32[]{:S(2)}) %all-to-all-start) | async-done | bytes 9437216 | tf_op jit(solution)/shard_map/all_to_all | solution.py:47
  293.9 5.1 all-to-all-start.1
  299.0 8.5 %copy.28 = bf16[192,8,8,384]{3,2,0,1:T(8,128)(2,1)} copy(bf16[192,8,8,384]{3,2,1,0:T(8,128)(2,1)} %bitcast.30) | data formatting | bytes 18874368 | tf_op jit(solution)/shard_map/all_to_all | solution.py:49
  307.4 195.9 %all-to-all-done.1 = bf16[1536,8,384]{2,0,1:T(8,128)(2,1)} async-done(((bf16[1536,8,384]{2,0,1:T(8,128)(2,1)}), bf16[1536,8,384]{2,0,1:T(8,128)(2,1)}, u32[]{:S(2)}, u32[]{:S(2)}) %all-to-all-start.1) | async-done | bytes 9437216 | tf_op jit(solution)/shard_map/all_to_all | solution.py:48
  503.3 5.1 all-to-all-start.2
  508.4 0.7 dynamic_slice.9
  509.1 0.7 dynamic_slice.10
  509.7 0.7 dynamic_slice.11
  510.4 202.7 %all-to-all-done.2 = bf16[1536,8,384]{2,0,1:T(8,128)(2,1)} async-done(((bf16[1536,8,384]{2,0,1:T(8,128)(2,1)}), bf16[1536,8,384]{2,0,1:T(8,128)(2,1)}, u32[]{:S(2)}, u32[]{:S(2)}) %all-to-all-start.2) | async-done | bytes 9437216 | tf_op jit(solution)/shard_map/all_to_all | solution.py:49
  713.1 9.3 %copy.34 = bf16[12288,384]{1,0:T(8,128)(2,1)} copy(bf16[12288,384]{1,0:T(8,128)(2,1)} %bitcast.1) | data formatting | bytes 18874368
  722.4 9.3 %copy.35 = bf16[12288,384]{1,0:T(8,128)(2,1)} copy(bf16[12288,384]{1,0:T(8,128)(2,1)} %bitcast.3) | data formatting | bytes 18874368
  731.7 9.3 %copy.36 = bf16[12288,384]{1,0:T(8,128)(2,1)} copy(bf16[12288,384]{1,0:T(8,128)(2,1)} %bitcast.5) | data formatting | bytes 18874368
  (12 shorter events, 0.0 us)
Async XLA Ops:
  0.6 0.9 copy-start
  0.7 14.4 %copy-start.3 = (f32[1536]{0:T(1024)S(1)}, f32[1536]{0:T(1024)}, u32[]{:S(2)}) copy-start(f32[1536]{0:T(1024)} %param.19) | copy-start | bytes 18436
  0.7 14.4 %copy-start.4 = (bf16[1536,16]{0,1:T(8,128)(2,1)S(1)}, bf16[1536,16]{0,1:T(8,128)(2,1)}, u32[]{:S(2)}) copy-start(bf16[1536,16]{0,1:T(8,128)(2,1)} %param.14) | copy-start | bytes 147460
  0.7 14.4 %copy-start.6 = (bf16[16,3072]{1,0:T(8,128)(2,1)S(1)}, bf16[16,3072]{1,0:T(8,128)(2,1)}, u32[]{:S(2)}) copy-start(bf16[16,3072]{1,0:T(8,128)(2,1)} %param.15) | copy-start | bytes 294916
  0.7 14.4 %copy-start.2 = (bf16[1536,3072]{1,0:T(8,128)(2,1)S(1)}, bf16[1536,3072]{1,0:T(8,128)(2,1)}, u32[]{:S(2)}) copy-start(bf16[1536,3072]{1,0:T(8,128)(2,1)} %param.13) | copy-start | bytes 28311556
  1.5 21.5 %slice-start = ((s8[9437184]{0:T(1024)(128)(4,1)}), s8[4194304]{0:T(1024)(128)(4,1)S(1)}, s32[]{:S(2)}) async-start(s8[9437184]{0:T(1024)(128)(4,1)} %bitcast.33), calls=%async_computation.3 | async-start | bytes 8388608
  1.5 21.5 %slice-start.1 = ((s8[9437184]{0:T(1024)(128)(4,1)}), s8[4194304]{0:T(1024)(128)(4,1)S(1)}, s32[]{:S(2)}) async-start(s8[9437184]{0:T(1024)(128)(4,1)} %bitcast.33), calls=%async_computation.4 | async-start | bytes 8388608
  15.1 8.0 %slice-start.2 = ((s8[9437184]{0:T(1024)(128)(4,1)}), s8[1048576]{0:T(1024)(128)(4,1)S(1)}, s32[]{:S(2)}) async-start(s8[9437184]{0:T(1024)(128)(4,1)} %bitcast.33), calls=%async_computation.5 | async-start | bytes 2097152
  15.1 8.0 %copy-start.5 = (bf16[1536,16]{0,1:T(8,128)(2,1)S(1)}, bf16[1536,16]{0,1:T(8,128)(2,1)}, u32[]{:S(2)}) copy-start(bf16[1536,16]{0,1:T(8,128)(2,1)} %param.17) | copy-start | bytes 147460
  15.1 8.0 %copy-start.7 = (bf16[16,3072]{1,0:T(8,128)(2,1)S(1)}, bf16[16,3072]{1,0:T(8,128)(2,1)}, u32[]{:S(2)}) copy-start(bf16[16,3072]{1,0:T(8,128)(2,1)} %param.18) | copy-start | bytes 294916
  90.2 203.7 %all-to-all-start = ((bf16[1536,8,384]{2,0,1:T(8,128)(2,1)}), bf16[1536,8,384]{2,0,1:T(8,128)(2,1)}, u32[]{:S(2)}, u32[]{:S(2)}) async-start(bf16[1536,8,384]{2,0,1:T(8,128)(2,1)} %bitcast.28), calls=%async_computation | async-start | bytes 18874368 | tf_op jit(solution)/shard_map/all_to_all | solution.py:47
  293.9 209.4 %all-to-all-start.1 = ((bf16[1536,8,384]{2,0,1:T(8,128)(2,1)}), bf16[1536,8,384]{2,0,1:T(8,128)(2,1)}, u32[]{:S(2)}, u32[]{:S(2)}) async-start(bf16[1536,8,384]{2,0,1:T(8,128)(2,1)} %bitcast.29), calls=%async_computation.1 | async-start | bytes 18874368 | tf_op jit(solution)/shard_map/all_to_all | solution.py:48
  503.3 209.7 %all-to-all-start.2 = ((bf16[1536,8,384]{2,0,1:T(8,128)(2,1)}), bf16[1536,8,384]{2,0,1:T(8,128)(2,1)}, u32[]{:S(2)}, u32[]{:S(2)}) async-start(bf16[1536,8,384]{2,0,1:T(8,128)(2,1)} %bitcast.27), calls=%async_computation.2 | async-start | bytes 18874368 | tf_op jit(solution)/shard_map/all_to_all | solution.py:49
  713.1 27.9 %copy-start.1 = (bf16[16,3072]{1,0:T(8,128)(2,1)S(1)}, bf16[16,3072]{1,0:T(8,128)(2,1)}, u32[]{:S(2)}) copy-start(bf16[16,3072]{1,0:T(8,128)(2,1)} %param.12) | copy-start | bytes 294916
where the time goes:
time: 742 us; the launch traced here: 741 us
  waiting for transfers between devices  569 us (77%)
  local copies, waits for them, and re-layouts  56 us (8%)
  blocking collectives  39.2 us (5%)
  other arithmetic  31.9 us (4%)
  matrix products  29.4 us (4%)
  starting transfers between devices  15.2 us (2%)
    all_to_all x1, waiting for transfers between devices, on_device(): lax.all_to_all(narrow_value, 'shard', split_axis=1, concat_axis=0, tiled=...  203 us
    all_to_all x1, waiting for transfers between devices, on_device(): lax.all_to_all(narrow_key, 'shard', split_axis=1, concat_axis=0, tiled=True)  196 us
    all_to_all x1, waiting for transfers between devices, on_device(): lax.all_to_all(narrow_query, 'shard', split_axis=1, concat_axis=0, tiled=...  170 us
    pmax x1, blocking collectives, on_device(): lax.pmax((jnp.max(jnp.abs(result_gained_query), axis=0), jnp.max(jnp.abs(...  39.2 us
    unnamed x25, local copies, waits for them, and re-layouts  28.8 us
    convert_element_type x1, other arithmetic, on_device(): (result_gained_value / scale_value).astype(jnp.bfloat16)  20.3 us
  transfers between devices with their start and end apart: 3, of which 3 were waited for; matrix products, arithmetic and copies ran while one was open for 5% of the time, Pallas kernels for 0%

commit v1 on v0

v1 whole, which is shorter than its diff:
```python
import functools

import jax
import jax.numpy as jnp
from jax import lax
from jax.experimental import pallas as pl
from jax.experimental.pallas import tpu as pltpu
from jax.sharding import PartitionSpec as P


mix_rate = 1.0
LANES = 128
PIECES = 16
SLOTS, AHEAD = 8, 4


def on_device_plain(
    w_query,
    low_query,
    high_query,
    w_key,
    low_key,
    high_key,
    w_value,
    low_value,
    high_value,
    norm_gain,
):
    def gained(w, low, high):
        delta = mix_rate * jnp.dot(low, high, preferred_element_type=jnp.float32)
        return (w.astype(jnp.float32) + delta) * norm_gain[:, None]

    gains = (
        gained(w_query, low_query, high_query),
        gained(w_key, low_key, high_key),
        gained(w_value, low_value, high_value),
    )
    scales = lax.pmax(tuple(jnp.max(jnp.abs(g), axis=0) for g in gains), "shard")
    finals = tuple(
        lax.all_to_all(
            (g / s).astype(jnp.bfloat16), "shard", split_axis=1, concat_axis=0, tiled=True
        )
        for g, s in zip(gains, scales)
    )
    width = finals[0].shape[1]
    start = lax.axis_index("shard") * width
    return finals + tuple(lax.dynamic_slice_in_dim(s, start, width) for s in scales)


def pack_kernel(jobs, *refs):
    out_ref, held, in_sem, out_sem = refs[-4:]

    def fetch(j):
        which, column, width, _, _ = jobs[j]
        w_ref = refs[which]
        return pltpu.make_async_copy(
            w_ref.at[:, pl.ds(column, width)],
            held.at[j % SLOTS, :, pl.ds(0, width)],
            in_sem.at[j % SLOTS],
        )

    def put(j):
        _, _, width, dest, at = jobs[j]
        rows = held.shape[1]
        return pltpu.make_async_copy(
            held.at[j % SLOTS, :, pl.ds(0, width)],
            out_ref.at[pl.ds(dest * rows, rows), pl.ds(at, width)],
            out_sem.at[j % SLOTS],
        )

    count = len(jobs)
    for j in range(count + AHEAD):
        if j < count:
            if j >= SLOTS:
                put(j - SLOTS).wait()
            fetch(j).start()
        if j >= AHEAD:
            fetch(j - AHEAD).wait()
            put(j - AHEAD).start()
    for j in range(max(0, count - SLOTS), count):
        put(j).wait()


def pack(weights, parts, n):
    rows, columns = weights[0].shape
    block = columns // n
    total = sum(width for _, _, width in parts)
    widest = max(width for _, _, width in parts)
    jobs = []
    for dest in range(n):
        at = 0
        for which, first, width in parts:
            jobs.append((which, dest * block + first, width, dest, at))
            at += width
    return pl.pallas_call(
        functools.partial(pack_kernel, tuple(jobs)),
        out_shape=jax.ShapeDtypeStruct((n * rows, total), weights[0].dtype),
        in_specs=[pl.BlockSpec(memory_space=pl.ANY)] * len(weights),
        out_specs=pl.BlockSpec(memory_space=pl.ANY),
        scratch_shapes=[
            pltpu.VMEM((SLOTS, rows, widest), weights[0].dtype),
            pltpu.SemaphoreType.DMA((SLOTS,)),
            pltpu.SemaphoreType.DMA((SLOTS,)),
        ],
        cost_estimate=pl.CostEstimate(
            flops=0, bytes_accessed=4 * n * rows * total, transcendentals=0
        ),
    )(*weights)


def merge_kernel(steps, raw_ref, left_ref, right_ref, *refs):
    out_ref, scale_ref, merged, peak = refs[-4:]
    step = pl.program_id(1)
    rows = raw_ref.shape[0]
    sub = 256 if rows % 256 == 0 else rows
    top = jnp.zeros((1, LANES), jnp.float32)
    for i in range(rows // sub):
        both = lax.dot_general(
            left_ref[:, i * sub : (i + 1) * sub],
            right_ref[...],
            (((0,), (0,)), ((), ())),
            preferred_element_type=jnp.float32,
        )
        delta, gain = both[:, :LANES], both[:, LANES:]
        base = raw_ref[i * sub : (i + 1) * sub, :].astype(jnp.float32)
        gained = (base + mix_rate * delta) * gain
        merged[pl.ds(pl.multiple_of(step * rows + i * sub, sub), sub), :] = gained
        top = jnp.maximum(top, jnp.max(jnp.abs(gained), axis=0, keepdims=True))
    so_far = jnp.where(step == 0, top, jnp.maximum(top, peak[0:1, :]))
    peak[0:1, :] = so_far

    @pl.when(step == steps - 1)
    def _():
        scale_ref[...] = so_far
        inverse = 1.0 / so_far

        @pl.loop(0, merged.shape[0] // sub)
        def _(i):
            here = pl.ds(pl.multiple_of(i * sub, sub), sub)
            out_ref[here, :] = (merged[here, :] * inverse).astype(out_ref.dtype)


def merge(raw, raw_tile, tiles, out_tile, columns, left, right, steps, earlier=()):
    height = raw.shape[0]
    rows, depth = height // steps, left.shape[0]
    return pl.pallas_call(
        functools.partial(merge_kernel, steps),
        grid=(tiles, steps),
        out_shape=(
            jax.ShapeDtypeStruct((height, columns), jnp.bfloat16),
            jax.ShapeDtypeStruct((1, columns), jnp.float32),
        ),
        in_specs=[
            pl.BlockSpec((rows, LANES), lambda t, s: (s, raw_tile + t)),
            pl.BlockSpec((depth, rows), lambda t, s: (0, s)),
            pl.BlockSpec((depth, 2 * LANES), lambda t, s: (0, out_tile + t)),
        ]
        + [pl.BlockSpec(memory_space=pl.ANY)] * len(earlier),
        out_specs=(
            pl.BlockSpec((height, LANES), lambda t, s: (0, out_tile + t)),
            pl.BlockSpec((1, LANES), lambda t, s: (0, out_tile + t)),
        ),
        scratch_shapes=[
            pltpu.VMEM((height, LANES), jnp.float32),
            pltpu.VMEM((8, LANES), jnp.float32),
        ],
        input_output_aliases={3 + i: i for i in range(len(earlier))},
        compiler_params=pltpu.CompilerParams(
            dimension_semantics=("arbitrary", "arbitrary"), vmem_limit_bytes=40 * 2**20
        ),
        cost_estimate=pl.CostEstimate(
            flops=4 * height * tiles * LANES * depth,
            bytes_accessed=4 * height * tiles * LANES,
            transcendentals=0,
        ),
    )(raw, left, right, *earlier)


def split_gain(gain):
    first = lax.reduce_precision(gain, 8, 7)
    second = lax.reduce_precision(gain - first, 8, 7)
    third = lax.reduce_precision(gain - first - second, 8, 7)
    return jnp.stack([first, second, third]).astype(jnp.bfloat16)


def gather_left(lows, norm_gain, n, m):
    rows, rank = lows[0].shape
    own = jnp.concatenate([low.T for low in lows] + [split_gain(norm_gain)], axis=0)
    count = len(lows) * rank
    lines = count + PIECES
    own = jnp.pad(own, ((0, lines - own.shape[0]), (0, 0)))
    part = rows // m
    mine = lax.dynamic_slice_in_dim(own, lax.axis_index("model") * part, part, axis=1)
    mine = lax.all_gather(mine, "shard")
    half = lines // 2
    every = jnp.concatenate(
        [lax.all_gather(mine[:, :half], "model"), lax.all_gather(mine[:, half:], "model")], axis=2
    )
    every = every.transpose(2, 1, 0, 3).reshape(lines, n * rows)
    return [
        jnp.concatenate([every[i * rank : (i + 1) * rank], every[count:]], axis=0)
        for i in range(len(lows))
    ]


def make_right(high, place, width):
    rank, tiles = high.shape[0], width // LANES
    mine = lax.dynamic_slice_in_dim(high, place * width, width, axis=1)
    mine = mine.reshape(rank, tiles, LANES)
    ones = (jnp.arange(PIECES) < 3).astype(high.dtype)[:, None, None]
    ones = jnp.broadcast_to(ones, (PIECES, tiles, LANES))
    top = jnp.concatenate([mine, jnp.zeros_like(mine)], axis=2)
    bottom = jnp.concatenate([jnp.zeros_like(ones), ones], axis=2)
    return jnp.concatenate([top, bottom], axis=0).reshape(rank + PIECES, 2 * width)


def on_device(
    n,
    m,
    w_query,
    low_query,
    high_query,
    w_key,
    low_key,
    high_key,
    w_value,
    low_value,
    high_value,
    norm_gain,
):
    width = w_query.shape[1] // n
    tiles = width // LANES
    place = lax.axis_index("shard")

    def exchange(packed):
        return lax.all_to_all(packed, "shard", split_axis=0, concat_axis=0, tiled=True)

    first = exchange(pack((w_query,), ((0, 0, LANES),), n))
    rest = width - LANES
    bulk = exchange(
        pack(
            (w_query, w_key, w_value),
            ((0, LANES, rest), (1, 0, width), (2, 0, rest)),
            n,
        ),
    )
    last = exchange(pack((w_value,), ((0, rest, LANES),), n))

    left_query, left_key, left_value = gather_left(
        (low_query, low_key, low_value), norm_gain, n, m
    )
    right_query = make_right(high_query, place, width)
    right_key = make_right(high_key, place, width)
    right_value = make_right(high_value, place, width)

    query = merge(first, 0, 1, 0, width, left_query, right_query, n)
    query = merge(bulk, 0, tiles - 1, 1, width, left_query, right_query, n, query)
    key = merge(bulk, tiles - 1, tiles, 0, width, left_key, right_key, n)
    value = merge(bulk, 2 * tiles - 1, tiles - 1, 0, width, left_value, right_value, n)
    value = merge(last, 0, 1, tiles - 1, width, left_value, right_value, n, value)
    finals, scales = zip(query, key, value)
    return finals + tuple(s.reshape(width) for s in scales)


def solution(mesh):
    n, m = mesh.shape["shard"], mesh.shape["model"]

    def chosen(*args):
        rows, columns = args[0].shape
        aligned = columns % (n * LANES) == 0 and columns // n >= 2 * LANES
        if aligned and rows % (m * LANES) == 0:
            return on_device(n, m, *args)
        return on_device_plain(*args)

    return jax.shard_map(
        chosen,
        mesh=mesh,
        in_specs=(
            P("shard", "model"),
            P("shard", None),
            P(None, "model"),
            P("shard", "model"),
            P("shard", None),
            P(None, "model"),
            P("shard", "model"),
            P("shard", None),
            P(None, "model"),
            P("shard"),
        ),
        out_specs=(
            P(None, ("model", "shard")),
            P(None, ("model", "shard")),
            P(None, ("model", "shard")),
            P(("model", "shard")),
            P(("model", "shard")),
            P(("model", "shard")),
        ),
        check_vma=False,
    )
```

time: 742 us -> 706 us (0.951)
  waiting for transfers between devices: 569 us -> 60.6 us
  blocking collectives: 39.2 us -> 508 us
  Pallas kernels: 0 us -> 91.7 us
  local copies, waits for them, and re-layouts: 56 us -> 21.4 us
  matrix products: 29.4 us -> 0 us
  other arithmetic: 31.9 us -> 4.25 us
    all_to_all x3, waiting for transfers between devices: 569 us -> 60.6 us  [exchange(): lax.all_to_all(packed, 'shard', split_axis=0, concat_axis=0, tiled=True)]
    all_gather x0 -> x3, blocking collectives: none -> 508 us  [the longest x1 490 us: gather_left(): mine = lax.all_gather(mine, 'shard')]
    pallas_call x0 -> x8, Pallas kernels: none -> 91.7 us  [the longest x5 67.8 us: merge(): pl.pallas_call(functools.partial(merge_kernel, steps), grid=(tiles, steps...]
    pmax x1 -> x0, blocking collectives: 39.2 us -> none  [on_device(): lax.pmax((jnp.max(jnp.abs(result_gained_query), axis=0), jnp.max(jnp.abs(...]
    convert_element_type x2 -> x1, other arithmetic: 31.9 us -> 0.01 us  [make_right(): ones = (jnp.arange(PIECES) < 3).astype(high.dtype)[:, None, None]]
    dot_general x3 -> x0, matrix products: 29.4 us -> none  [the longest x1 13.5 us: on_device(): jnp.dot(low_query, high_query, preferred_element_type=jnp.float32)]
    unnamed x25 -> x26, local copies, waits for them, and re-layouts: 28.8 us -> 2.43 us
    all_to_all x3 -> x0, local copies, waits for them, and re-layouts: 25.3 us -> none  [the longest x1 8.45 us: on_device(): lax.all_to_all(narrow_value, 'shard', split_axis=1, concat_axis=0, tiled=...]
  transfers between devices with their start and end apart: 3 -> 3, of which waited for: 3 -> 2; matrix products, arithmetic and copies ran while one was open for 5% -> 3% of each run, Pallas kernels for 0% -> 6%
where the time goes in v1:
time: 706 us; the launch traced here: 705 us
  blocking collectives  508 us (72%)
  Pallas kernels  91.7 us (13%)
  waiting for transfers between devices  60.6 us (9%)
  local copies, waits for them, and re-layouts  21.4 us (3%)
  starting transfers between devices  18 us (3%)
    all_gather x1, blocking collectives, gather_left(): mine = lax.all_gather(mine, 'shard')  490 us
    pallas_call x5, Pallas kernels, merge(): pl.pallas_call(functools.partial(merge_kernel, steps), grid=(tiles, steps...  67.8 us
    all_to_all x3, waiting for transfers between devices, exchange(): lax.all_to_all(packed, 'shard', split_axis=0, concat_axis=0, tiled=True)  60.6 us
    pallas_call x3, Pallas kernels, pack(): pl.pallas_call(functools.partial(pack_kernel, tuple(jobs)), out_shape=jax...  23.8 us
    all_to_all x3, starting transfers between devices, exchange(): lax.all_to_all(packed, 'shard', split_axis=0, concat_axis=0, tiled=True)  18 us
  transfers between devices with their start and end apart: 3, of which 2 were waited for; matrix products, arithmetic and copies ran while one was open for 3% of the time, Pallas kernels for 6%

profile of v1, /device:TPU:0, one launch (start us, length us, event | category | flops | bytes accessed | tf_op | source)
XLA Modules:
  0.0 704.6 jit_solution(7821658933308625169)
XLA Ops:
  0.6 3.9 shard_map.146
  4.6 7.3 %all-to-all-start.1 = ((bf16[8,1536,128]{2,1,0:T(8,128)(2,1)}), bf16[8,1536,128]{2,1,0:T(8,128)(2,1)S(1)}, u32[]{:S(2)}, u32[]{:S(2)}) async-start(bf16[8,1536,128]{2,1,0:T(8,128)(2,1)} %bitcast.28), calls=%async_computation.1 | async-start | bytes 6291456 | tf_op jit(solution)/shard_map/all_to_all | solution.py:236
  11.9 16.0 %shard_map.145 = bf16[12288,896]{1,0:T(8,128)(2,1)} custom-call(bf16[1536,3072]{1,0:T(8,128)(2,1)} %refs_0_.4, bf16[1536,3072]{1,0:T(8,128)(2,1)} %refs_1_.1, bf16[1536,3072]{1,0:T(8,128)(2,1)} %refs_0_.5), custom_call_target="tpu_custom_call" | custom-call | bytes 44040192 | tf_op jit(solution)/shard_map/pallas_call | solution.py:95
  27.9 54.7 %all-to-all-done.1 = bf16[8,1536,128]{2,1,0:T(8,128)(2,1)S(1)} async-done(((bf16[8,1536,128]{2,1,0:T(8,128)(2,1)}), bf16[8,1536,128]{2,1,0:T(8,128)(2,1)S(1)}, u32[]{:S(2)}, u32[]{:S(2)}) %all-to-all-start.1) | async-done | bytes 3145760 | tf_op jit(solution)/shard_map/all_to_all | solution.py:236
  82.6 6.2 all-to-all-start
  88.9 3.9 shard_map.150
  92.9 0.9 concatenate.39
  93.8 490.3 %all-gather = bf16[512,384]{1,0:T(8,128)(2,1)S(1)} all-gather(bf16[64,384]{1,0:T(8,128)(2,1)S(1)} %pad_dynamic-slice_fusion), channel_id=2, replica_groups=mesh['shard'=8,'model'=4] {'shard'}, dimensions={0}, use_global_device_ids=true | all-gather | bytes 442368 | tf_op jit(solution)/shard_map/all_gather | solution.py:194
  584.1 0.7 fusion.10
  584.8 4.5 all-to-all-start.2
  589.3 8.8 %all-gather.1 = bf16[32,32,384]{2,1,0:T(8,128)(2,1)S(1)} all-gather(bf16[8,32,384]{2,1,0:T(8,128)(2,1)} %get-tuple-element.32), channel_id=3, replica_groups=mesh['shard'=8,'model'=4] {'model'}, dimensions={0}, use_global_device_ids=true | all-gather | bytes 983040 | tf_op jit(solution)/shard_map/all_gather | solution.py:197
  598.1 8.7 %all-gather.2 = bf16[32,32,384]{2,1,0:T(8,128)(2,1)S(1)} all-gather(bf16[8,32,384]{2,1,0:T(8,128)(2,1)S(1)} %get-tuple-element.33), channel_id=4, replica_groups=mesh['shard'=8,'model'=4] {'model'}, dimensions={0}, use_global_device_ids=true | all-gather | bytes 983040 | tf_op jit(solution)/shard_map/all_gather | solution.py:197
  607.1 1.1 fusion.9
  608.1 1.1 copy.24
  609.2 2.1 slice.35
  611.2 2.0 copy.27
  613.3 2.0 slice.41
  615.3 2.0 copy.25
  617.4 2.0 slice.37
  619.4 0.7 constant_dynamic-slice_fusion
  620.4 2.1 copy.26
  622.4 2.0 slice.39
  624.5 1.2 constant_dynamic-update-slice_fusion.1
  625.7 2.1 pad_maximum_fusion.left_ref
  627.9 5.8 shard_map.147
  633.7 15.5 %shard_map.151 = (bf16[12288,384]{1,0:T(8,128)(2,1)}, f32[1,384]{1,0:T(1,128)S(1)}) custom-call(bf16[12288,896]{1,0:T(8,128)(2,1)} %bitcast.1.raw_ref, bf16[32,12288]{1,0:T(8,128)(2,1)S(1)} %get-tuple-element.30.left_ref, bf16[32,768]{1,0:T(8,128)(2,1)S(1)} %bitcast.21), custom_call_target="tpu_custom_call" | custom-call | flops 402653184 | bytes 12582912 | tf_op jit(solution)/shard_map/pallas_call | solution.py:146
  649.2 5.9 all-to-all-done.2
  655.1 1.1 copy-done.3
  656.2 8.5 %shard_map.152 = (bf16[12288,384]{1,0:T(8,128)(2,1)}, f32[1,384]{1,0:T(1,128)S(1)}) custom-call(bf16[12288,128]{1,0:T(8,128)(2,1)} %bitcast.12.raw_ref, bf16[32,12288]{1,0:T(8,128)(2,1)S(1)} %copy-done.3, bf16[32,768]{1,0:T(8,128)(2,1)S(1)} %bitcast.22, bf16[12288,384]{1,0:T(8,128)(2,1)} %get-tuple-element.20.refs_0_, ...), custom_call_target="tpu_custom_call", output_to_operand_aliasing={{0}: (3, {}), {1}: (4, {})} | custom-call | flops 201326592 | bytes 6291456 | tf_op jit(solution)/shard_map/pallas_call | solution.py:146
  664.7 0.6 reduce.2
  665.3 15.6 %shard_map.148 = (bf16[12288,384]{1,0:T(8,128)(2,1)}, f32[1,384]{1,0:T(1,128)S(1)}) custom-call(bf16[12288,896]{1,0:T(8,128)(2,1)} %bitcast.1.raw_ref, bf16[32,12288]{1,0:T(8,128)(2,1)S(1)} %copy-done.5, bf16[32,768]{1,0:T(8,128)(2,1)S(1)} %bitcast.24, bf16[12288,384]{1,0:T(8,128)(2,1)} %get-tuple-element.16.refs_0_, ...), custom_call_target="tpu_custom_call", output_to_operand_aliasing={{0}: (3, {}), {1}: (4, {})} | custom-call | flops 402653184 | bytes 12582912 | tf_op jit(solution)/shard_map/pallas_call | solution.py:146
  681.5 22.5 %shard_map.149 = (bf16[12288,384]{1,0:T(8,128)(2,1)}, f32[1,384]{1,0:T(1,128)S(1)}) custom-call(bf16[12288,896]{1,0:T(8,128)(2,1)} %bitcast.1.raw_ref, bf16[32,12288]{1,0:T(8,128)(2,1)S(1)} %copy-done.6, bf16[32,768]{1,0:T(8,128)(2,1)S(1)} %bitcast.25), custom_call_target="tpu_custom_call" | custom-call | flops 603979776 | bytes 18874368 | tf_op jit(solution)/shard_map/pallas_call | solution.py:146
  (41 shorter events, 1.8 us)
Async XLA Ops:
  0.6 619.5 %copy-start = (bf16[16,3072]{1,0:T(8,128)(2,1)S(1)}, bf16[16,3072]{1,0:T(8,128)(2,1)}, u32[]{:S(2)}) copy-start(bf16[16,3072]{1,0:T(8,128)(2,1)} %param.12) | copy-start | bytes 294916
  4.6 78.0 %all-to-all-start.1 = ((bf16[8,1536,128]{2,1,0:T(8,128)(2,1)}), bf16[8,1536,128]{2,1,0:T(8,128)(2,1)S(1)}, u32[]{:S(2)}, u32[]{:S(2)}) async-start(bf16[8,1536,128]{2,1,0:T(8,128)(2,1)} %bitcast.28), calls=%async_computation.1 | async-start | bytes 6291456 | tf_op jit(solution)/shard_map/all_to_all | solution.py:236
  82.6 502.2 %all-to-all-start = ((bf16[8,1536,896]{2,1,0:T(8,128)(2,1)}), bf16[8,1536,896]{2,1,0:T(8,128)(2,1)}, u32[]{:S(2)}, u32[]{:S(2)}) async-start(bf16[8,1536,896]{2,1,0:T(8,128)(2,1)} %bitcast.26), calls=%async_computation | async-start | bytes 44040192 | tf_op jit(solution)/shard_map/all_to_all | solution.py:236
  88.8 4.0 copy-start.10
  88.8 4.0 copy-start.8
  88.8 4.0 copy-start.9
  584.8 70.3 %all-to-all-start.2 = ((bf16[8,1536,128]{2,1,0:T(8,128)(2,1)}), bf16[8,1536,128]{2,1,0:T(8,128)(2,1)}, u32[]{:S(2)}, u32[]{:S(2)}) async-start(bf16[8,1536,128]{2,1,0:T(8,128)(2,1)} %bitcast.27), calls=%async_computation.2 | async-start | bytes 6291456 | tf_op jit(solution)/shard_map/all_to_all | solution.py:236
  624.5 3.4 copy-start.7
  627.9 5.8 copy-start.4
  627.9 5.8 copy-start.2
  655.1 1.1 copy-start.3
  656.2 9.1 %copy-start.5 = (bf16[32,12288]{1,0:T(8,128)(2,1)S(1)}, bf16[32,12288]{1,0:T(8,128)(2,1)}, u32[]{:S(2)}) copy-start(bf16[32,12288]{1,0:T(8,128)(2,1)} %copy-done.4) | copy-start | bytes 2359300
  665.3 16.2 %copy-start.6 = (bf16[32,12288]{1,0:T(8,128)(2,1)S(1)}, bf16[32,12288]{1,0:T(8,128)(2,1)}, u32[]{:S(2)}) copy-start(bf16[32,12288]{1,0:T(8,128)(2,1)} %pad_maximum_fusion.left_ref) | copy-start | bytes 2359300
  681.5 23.1 %copy-start.1 = (bf16[16,3072]{1,0:T(8,128)(2,1)S(1)}, bf16[16,3072]{1,0:T(8,128)(2,1)}, u32[]{:S(2)}) copy-start(bf16[16,3072]{1,0:T(8,128)(2,1)} %param.12) | copy-start | bytes 294916

commit v2 on v1

--- a/solution.py
+++ b/solution.py
@@ -193,9 +193,9 @@
     mine = lax.dynamic_slice_in_dim(own, lax.axis_index("model") * part, part, axis=1)
     mine = lax.all_gather(mine, "shard")
     half = lines // 2
-    every = jnp.concatenate(
-        [lax.all_gather(mine[:, :half], "model"), lax.all_gather(mine[:, half:], "model")], axis=2
-    )
+    halves = mine[:, :half], mine[:, half:]
+    halves = [lax.all_gather(one, "model") for one in halves]
+    every = jnp.concatenate(halves, axis=2)
     every = every.transpose(2, 1, 0, 3).reshape(lines, n * rows)
     return [
         jnp.concatenate([every[i * rank : (i + 1) * rank], every[count:]], axis=0)
@@ -237,13 +237,12 @@
 
     first = exchange(pack((w_query,), ((0, 0, LANES),), n))
     rest = width - LANES
-    bulk = exchange(
-        pack(
-            (w_query, w_key, w_value),
-            ((0, LANES, rest), (1, 0, width), (2, 0, rest)),
-            n,
-        ),
-    )
+    packed = pack(
+        (w_query, w_key, w_value),
+        ((0, LANES, rest), (1, 0, width), (2, 0, rest)),
+        n,
+    )
+    bulk = exchange(packed)
     last = exchange(pack((w_value,), ((0, rest, LANES),), n))
 
     left_query, left_key, left_value = gather_left(

time: 706 us -> 706 us (level)
  no operation moved by 1% of the time
where the time goes in v2:
time: 706 us; the launch traced here: 705 us
  blocking collectives  508 us (72%)
  Pallas kernels  91.7 us (13%)
  waiting for transfers between devices  60.6 us (9%)
  local copies, waits for them, and re-layouts  21.4 us (3%)
  starting transfers between devices  18 us (3%)
    all_gather x1, blocking collectives, gather_left(): mine = lax.all_gather(mine, 'shard')  490 us
    pallas_call x5, Pallas kernels, merge(): pl.pallas_call(functools.partial(merge_kernel, steps), grid=(tiles, steps...  67.8 us
    all_to_all x3, waiting for transfers between devices, exchange(): lax.all_to_all(packed, 'shard', split_axis=0, concat_axis=0, tiled=True)  60.6 us
    pallas_call x3, Pallas kernels, pack(): pl.pallas_call(functools.partial(pack_kernel, tuple(jobs)), out_shape=jax...  23.8 us
    all_to_all x3, starting transfers between devices, exchange(): lax.all_to_all(packed, 'shard', split_axis=0, concat_axis=0, tiled=True)  18 us
    all_gather x2, blocking collectives, gather_left(): halves = [lax.all_gather(one, 'model') for one in halves]  17.5 us
  transfers between devices with their start and end apart: 3, of which 2 were waited for; matrix products, arithmetic and copies ran while one was open for 3% of the time, Pallas kernels for 6%

profile of v2, /device:TPU:0, one launch (start us, length us, event | category | flops | bytes accessed | tf_op | source)
XLA Modules:
  0.0 704.6 jit_solution(7821658933308625169)
XLA Ops:
  0.6 3.9 shard_map.146
  4.6 7.3 %all-to-all-start.1 = ((bf16[8,1536,128]{2,1,0:T(8,128)(2,1)}), bf16[8,1536,128]{2,1,0:T(8,128)(2,1)S(1)}, u32[]{:S(2)}, u32[]{:S(2)}) async-start(bf16[8,1536,128]{2,1,0:T(8,128)(2,1)} %bitcast.28), calls=%async_computation.1 | async-start | bytes 6291456 | tf_op jit(solution)/shard_map/all_to_all | solution.py:236
  11.9 16.0 %shard_map.145 = bf16[12288,896]{1,0:T(8,128)(2,1)} custom-call(bf16[1536,3072]{1,0:T(8,128)(2,1)} %refs_0_.4, bf16[1536,3072]{1,0:T(8,128)(2,1)} %refs_1_.1, bf16[1536,3072]{1,0:T(8,128)(2,1)} %refs_0_.5), custom_call_target="tpu_custom_call" | custom-call | bytes 44040192 | tf_op jit(solution)/shard_map/pallas_call | solution.py:95
  27.9 54.7 %all-to-all-done.1 = bf16[8,1536,128]{2,1,0:T(8,128)(2,1)S(1)} async-done(((bf16[8,1536,128]{2,1,0:T(8,128)(2,1)}), bf16[8,1536,128]{2,1,0:T(8,128)(2,1)S(1)}, u32[]{:S(2)}, u32[]{:S(2)}) %all-to-all-start.1) | async-done | bytes 3145760 | tf_op jit(solution)/shard_map/all_to_all | solution.py:236
  82.6 6.2 all-to-all-start
  88.9 3.9 shard_map.150
  92.9 0.9 concatenate.39
  93.8 490.3 %all-gather = bf16[512,384]{1,0:T(8,128)(2,1)S(1)} all-gather(bf16[64,384]{1,0:T(8,128)(2,1)S(1)} %pad_dynamic-slice_fusion), channel_id=2, replica_groups=mesh['shard'=8,'model'=4] {'shard'}, dimensions={0}, use_global_device_ids=true | all-gather | bytes 442368 | tf_op jit(solution)/shard_map/all_gather | solution.py:194
  584.1 0.7 fusion.10
  584.8 4.5 all-to-all-start.2
  589.3 8.8 %all-gather.1 = bf16[32,32,384]{2,1,0:T(8,128)(2,1)S(1)} all-gather(bf16[8,32,384]{2,1,0:T(8,128)(2,1)} %get-tuple-element.32), channel_id=3, replica_groups=mesh['shard'=8,'model'=4] {'model'}, dimensions={0}, use_global_device_ids=true | all-gather | bytes 983040 | tf_op jit(solution)/shard_map/all_gather | solution.py:197
  598.1 8.7 %all-gather.2 = bf16[32,32,384]{2,1,0:T(8,128)(2,1)S(1)} all-gather(bf16[8,32,384]{2,1,0:T(8,128)(2,1)S(1)} %get-tuple-element.33), channel_id=4, replica_groups=mesh['shard'=8,'model'=4] {'model'}, dimensions={0}, use_global_device_ids=true | all-gather | bytes 983040 | tf_op jit(solution)/shard_map/all_gather | solution.py:197
  607.1 1.1 fusion.9
  608.1 1.1 copy.24
  609.2 2.1 slice.35
  611.2 2.0 copy.27
  613.3 2.0 slice.41
  615.3 2.0 copy.25
  617.4 2.0 slice.37
  619.4 0.7 constant_dynamic-slice_fusion
  620.4 2.1 copy.26
  622.4 2.0 slice.39
  624.5 1.2 constant_dynamic-update-slice_fusion.1
  625.7 2.1 pad_maximum_fusion.left_ref
  627.9 5.8 shard_map.147
  633.7 15.5 %shard_map.151 = (bf16[12288,384]{1,0:T(8,128)(2,1)}, f32[1,384]{1,0:T(1,128)S(1)}) custom-call(bf16[12288,896]{1,0:T(8,128)(2,1)} %bitcast.1.raw_ref, bf16[32,12288]{1,0:T(8,128)(2,1)S(1)} %get-tuple-element.30.left_ref, bf16[32,768]{1,0:T(8,128)(2,1)S(1)} %bitcast.21), custom_call_target="tpu_custom_call" | custom-call | flops 402653184 | bytes 12582912 | tf_op jit(solution)/shard_map/pallas_call | solution.py:146
  649.2 5.9 all-to-all-done.2
  655.1 1.1 copy-done.3
  656.2 8.5 %shard_map.152 = (bf16[12288,384]{1,0:T(8,128)(2,1)}, f32[1,384]{1,0:T(1,128)S(1)}) custom-call(bf16[12288,128]{1,0:T(8,128)(2,1)} %bitcast.12.raw_ref, bf16[32,12288]{1,0:T(8,128)(2,1)S(1)} %copy-done.3, bf16[32,768]{1,0:T(8,128)(2,1)S(1)} %bitcast.22, bf16[12288,384]{1,0:T(8,128)(2,1)} %get-tuple-element.20.refs_0_, ...), custom_call_target="tpu_custom_call", output_to_operand_aliasing={{0}: (3, {}), {1}: (4, {})} | custom-call | flops 201326592 | bytes 6291456 | tf_op jit(solution)/shard_map/pallas_call | solution.py:146
  664.7 0.6 reduce.2
  665.3 15.6 %shard_map.148 = (bf16[12288,384]{1,0:T(8,128)(2,1)}, f32[1,384]{1,0:T(1,128)S(1)}) custom-call(bf16[12288,896]{1,0:T(8,128)(2,1)} %bitcast.1.raw_ref, bf16[32,12288]{1,0:T(8,128)(2,1)S(1)} %copy-done.5, bf16[32,768]{1,0:T(8,128)(2,1)S(1)} %bitcast.24, bf16[12288,384]{1,0:T(8,128)(2,1)} %get-tuple-element.16.refs_0_, ...), custom_call_target="tpu_custom_call", output_to_operand_aliasing={{0}: (3, {}), {1}: (4, {})} | custom-call | flops 402653184 | bytes 12582912 | tf_op jit(solution)/shard_map/pallas_call | solution.py:146
  681.5 22.5 %shard_map.149 = (bf16[12288,384]{1,0:T(8,128)(2,1)}, f32[1,384]{1,0:T(1,128)S(1)}) custom-call(bf16[12288,896]{1,0:T(8,128)(2,1)} %bitcast.1.raw_ref, bf16[32,12288]{1,0:T(8,128)(2,1)S(1)} %copy-done.6, bf16[32,768]{1,0:T(8,128)(2,1)S(1)} %bitcast.25), custom_call_target="tpu_custom_call" | custom-call | flops 603979776 | bytes 18874368 | tf_op jit(solution)/shard_map/pallas_call | solution.py:146
  (41 shorter events, 1.8 us)
Async XLA Ops:
  0.6 619.5 %copy-start = (bf16[16,3072]{1,0:T(8,128)(2,1)S(1)}, bf16[16,3072]{1,0:T(8,128)(2,1)}, u32[]{:S(2)}) copy-start(bf16[16,3072]{1,0:T(8,128)(2,1)} %param.12) | copy-start | bytes 294916
  4.6 78.0 %all-to-all-start.1 = ((bf16[8,1536,128]{2,1,0:T(8,128)(2,1)}), bf16[8,1536,128]{2,1,0:T(8,128)(2,1)S(1)}, u32[]{:S(2)}, u32[]{:S(2)}) async-start(bf16[8,1536,128]{2,1,0:T(8,128)(2,1)} %bitcast.28), calls=%async_computation.1 | async-start | bytes 6291456 | tf_op jit(solution)/shard_map/all_to_all | solution.py:236
  82.6 502.2 %all-to-all-start = ((bf16[8,1536,896]{2,1,0:T(8,128)(2,1)}), bf16[8,1536,896]{2,1,0:T(8,128)(2,1)}, u32[]{:S(2)}, u32[]{:S(2)}) async-start(bf16[8,1536,896]{2,1,0:T(8,128)(2,1)} %bitcast.26), calls=%async_computation | async-start | bytes 44040192 | tf_op jit(solution)/shard_map/all_to_all | solution.py:236
  88.8 4.0 copy-start.10
  88.8 4.0 copy-start.8
  88.8 4.0 copy-start.9
  584.8 70.3 %all-to-all-start.2 = ((bf16[8,1536,128]{2,1,0:T(8,128)(2,1)}), bf16[8,1536,128]{2,1,0:T(8,128)(2,1)}, u32[]{:S(2)}, u32[]{:S(2)}) async-start(bf16[8,1536,128]{2,1,0:T(8,128)(2,1)} %bitcast.27), calls=%async_computation.2 | async-start | bytes 6291456 | tf_op jit(solution)/shard_map/all_to_all | solution.py:236
  624.5 3.4 copy-start.7
  627.9 5.8 copy-start.4
  627.9 5.8 copy-start.2
  655.1 1.1 copy-start.3
  656.2 9.1 %copy-start.5 = (bf16[32,12288]{1,0:T(8,128)(2,1)S(1)}, bf16[32,12288]{1,0:T(8,128)(2,1)}, u32[]{:S(2)}) copy-start(bf16[32,12288]{1,0:T(8,128)(2,1)} %copy-done.4) | copy-start | bytes 2359300
  665.3 16.2 %copy-start.6 = (bf16[32,12288]{1,0:T(8,128)(2,1)S(1)}, bf16[32,12288]{1,0:T(8,128)(2,1)}, u32[]{:S(2)}) copy-start(bf16[32,12288]{1,0:T(8,128)(2,1)} %pad_maximum_fusion.left_ref) | copy-start | bytes 2359300
  681.5 23.1 %copy-start.1 = (bf16[16,3072]{1,0:T(8,128)(2,1)S(1)}, bf16[16,3072]{1,0:T(8,128)(2,1)}, u32[]{:S(2)}) copy-start(bf16[16,3072]{1,0:T(8,128)(2,1)} %param.12) | copy-start | bytes 294916
